TPU v7x, 32 devices: a whole 2x2x4 slice. The times are simulated.
32 devices in a mesh: dom: 4 (over z), feat: 8 (over y, x, core).
Axes of the slice: x: 2, y: 2, z: 4, core: 2. Of those that a mesh axis runs over, the one named last changes fastest.
Arguments:
- node_feats: bfloat16 [4096, 512], P('dom', 'feat'), may hold values from -6 to 6
- rel_weight: bfloat16 [4, 512, 512], replicated, may hold values from -0.25 to 0.25
- self_weight: bfloat16 [512, 512], replicated, may hold values from -0.25 to 0.25
- bias: float32 [512], replicated, may hold values from -3 to 3
- out_degree: int32 [4, 4096], P(None, 'dom'), may hold values from 0 to 63
- adjacency: int32 [4, 8, 64, 256, 256], P('dom', 'feat'), may hold values 0 or 1
- tile_index: int32 [4, 8, 64, 3], P('dom', 'feat'), may hold values from 0 to 15, as said below
- tile_count: int32 [4, 8], P('dom', 'feat'), may hold values from 1 to 64, as said below
Outputs:
- embedding: bfloat16 [4096, 512], P('dom', 'feat')
Inputs may be any that keep to these rules, and one draw needn't show every extreme that they name: `tile_index`: the three entries of a slot are a relation below 4, a destination block below 16 and a source block of the device's own group below 4; entries of slots beyond a device's count are arbitrary within the range. `tile_count`: some device holds exactly 64 live slots.
All inputs are finite; a program needn't handle non-finite values. No bound on the sum of `adjacency` on one device may be relied on, other than what follows from the above.
Results may differ from a plain program's by a relative error of at most 0.0049.
Values may be sent and summed in bfloat16 or wider, within the bound.
A program may use at most 128 MiB of HBM per device.

v0:
```python
import jax
import jax.numpy as jnp
from jax import lax
from jax.sharding import PartitionSpec as P


def body(node_feats, rel_weight, self_weight, bias, out_degree, adjacency, tile_index, tile_count):
    owned_nodes = node_feats.shape[0]
    column_count = node_feats.shape[1]
    hidden_width = rel_weight.shape[1]
    tile_size = adjacency.shape[-1]
    group_count = lax.axis_size("dom")
    column_start = lax.axis_index("feat") * column_count
    features = lax.all_gather(node_feats, "feat", axis=1, tiled=True)
    inv_degree = 1.0 / jnp.maximum(out_degree, 1).astype(jnp.float32)
    adjacency_tiles = adjacency[0, 0]
    tile_list = tile_index[0, 0]
    live_tiles = tile_count[0, 0]
    self_columns = lax.dynamic_slice_in_dim(self_weight, column_start, column_count, 1)
    bias_columns = lax.dynamic_slice_in_dim(bias, column_start, column_count, 0)
    self_term = (
        jnp.dot(features, self_columns, preferred_element_type=jnp.float32) + bias_columns[None, :]
    )

    def source_rows(relation, source):
        source_block = lax.dynamic_slice_in_dim(features, source * tile_size, tile_size, 0)
        relation_matrix = lax.dynamic_index_in_dim(rel_weight, relation, 0, keepdims=False)
        degree_factor = lax.dynamic_slice(
            inv_degree, (relation, source * tile_size), (1, tile_size)
        )[0]
        product = jnp.dot(source_block, relation_matrix, preferred_element_type=jnp.float32)
        return (product * degree_factor[:, None]).astype(jnp.bfloat16)

    def add_tile(slot_index, running):
        relation = tile_list[slot_index, 0]
        target = tile_list[slot_index, 1]
        source = tile_list[slot_index, 2]
        source_msg = source_rows(relation, source)
        tile_cells = lax.dynamic_index_in_dim(adjacency_tiles, slot_index, 0, keepdims=False)
        contribution = jnp.dot(
            tile_cells.astype(jnp.bfloat16), source_msg, preferred_element_type=jnp.float32
        )
        current = lax.dynamic_slice_in_dim(running, target * tile_size, tile_size, 0)
        return lax.dynamic_update_slice_in_dim(
            running, current + contribution, target * tile_size, 0
        )

    partial_value = jnp.zeros((group_count * owned_nodes, hidden_width), jnp.float32)
    partial_value = lax.fori_loop(0, live_tiles, add_tile, partial_value)
    narrowed = lax.psum_scatter(partial_value, "feat", scatter_dimension=1, tiled=True)
    reduced = lax.psum_scatter(narrowed, "dom", scatter_dimension=0, tiled=True)
    return (reduced + self_term).astype(jnp.bfloat16)


def solution(mesh):
    placed = (
        P("dom", "feat"),
        P(),
        P(),
        P(),
        P(None, "dom"),
        P("dom", "feat", None, None, None),
        P("dom", "feat", None, None),
        P("dom", "feat"),
    )
    return jax.shard_map(
        body, mesh=mesh, in_specs=placed, out_specs=P("dom", "feat"), check_vma=False
    )
```

profile of v0, /device:TPU:0, one launch (start us, length us, event | category | flops | bytes accessed | tf_op | source)
XLA Modules:
  0.0 705.8 jit_solution(10071429290400987194)
XLA Ops:
  8.7 26.6 %all-gather.2.cloned.1.call-done = bf16[1024,512]{0,1:T(8,128)(2,1)} async-done(((bf16[1024,64]{0,1:T(8,128)(2,1)}), bf16[1024,512]{0,1:T(8,128)(2,1)}) %all-gather.2.cloned.1.call-update) | async-done | bytes 1048592 | tf_op jit(solution)/shard_map/all_gather | solution.py:14
  35.4 4.3 broadcast_in_dim.4.clone
  39.6 235.9 %while.10 = (s32[]{:T(128)}, f32[4096,512]{0,1:T(8,128)}, s32[]{:T(128)}, s32[64,3]{0,1:T(4,128)S(1)}, s32[64,256,256]{2,1,0:T(8,128)}, /*index=5*/bf16[1024,512...) while((s32[]{:T(128)}, f32[4096,512]{0,1:T(8,128)}, ...), condition=%wide.region_1.2_spmd, body=%wide.region_0.1_spmd.sunk | while | flops 201785360 | bytes 6294889 | solution.py:49
  41.6 1.1 constant_dynamic-slice_fusion.7
  45.6 1.7 convolution_add_fusion.3
  50.3 1.1 constant_dynamic-slice_fusion.7
  54.3 1.6 convolution_add_fusion.3
  59.1 1.1 constant_dynamic-slice_fusion.7
  63.0 1.7 convolution_add_fusion.3
  67.8 1.1 constant_dynamic-slice_fusion.7
  71.7 1.7 convolution_add_fusion.3
  76.5 1.1 constant_dynamic-slice_fusion.7
  80.5 1.7 convolution_add_fusion.3
  85.2 1.1 constant_dynamic-slice_fusion.7
  89.1 1.7 convolution_add_fusion.3
  93.9 1.1 constant_dynamic-slice_fusion.7
  97.8 1.7 convolution_add_fusion.3
  102.6 1.1 constant_dynamic-slice_fusion.7
  106.6 1.7 convolution_add_fusion.3
  115.3 1.7 convolution_add_fusion.3
  120.0 1.1 constant_dynamic-slice_fusion.7
  124.0 1.7 convolution_add_fusion.3
  128.7 1.1 constant_dynamic-slice_fusion.7
  132.7 1.7 convolution_add_fusion.3
  137.4 1.1 constant_dynamic-slice_fusion.7
  141.4 1.6 convolution_add_fusion.3
  146.1 1.1 constant_dynamic-slice_fusion.7
  150.0 1.7 convolution_add_fusion.3
  154.8 1.1 constant_dynamic-slice_fusion.7
  158.8 1.7 convolution_add_fusion.3
  163.6 1.1 constant_dynamic-slice_fusion.7
  167.5 1.7 convolution_add_fusion.3
  172.3 1.1 constant_dynamic-slice_fusion.7
  176.2 1.6 convolution_add_fusion.3
  184.9 1.7 convolution_add_fusion.3
  193.6 1.7 convolution_add_fusion.3
  202.3 1.7 convolution_add_fusion.3
  211.0 1.7 convolution_add_fusion.3
  219.7 1.6 convolution_add_fusion.3
  228.4 1.7 convolution_add_fusion.3
  237.1 1.7 convolution_add_fusion.3
  245.9 1.6 convolution_add_fusion.3
  254.6 1.7 convolution_add_fusion.3
  263.4 1.6 convolution_add_fusion.3
  272.0 1.7 convolution_add_fusion.3
  275.6 392.1 %reduce-scatter.3.cloned.1.call-done = f32[4096,64]{0,1:T(8,128)} async-done(((f32[4096,512]{0,1:T(8,128)}), f32[4096,64]{0,1:T(8,128)}) %reduce-scatter.3.cloned.1.call-update) | async-done | bytes 1048592 | tf_op jit(solution)/shard_map/reduce_scatter | solution.py:50
  668.5 28.8 %reduce-scatter.5.cloned.1.call-done = f32[1024,64]{0,1:T(8,128)} async-done(((f32[4096,64]{0,1:T(8,128)}), f32[1024,64]{0,1:T(8,128)}) %reduce-scatter.5.cloned.1.call-update) | async-done | bytes 262160 | tf_op jit(solution)/shard_map/reduce_scatter | solution.py:51
  697.3 2.0 fusion.14
  (160 shorter events, 70.4 us)
Async XLA Ops:
  6.5 690.8 %copy-start = (bf16[512,512]{1,0:T(8,128)(2,1)S(1)}, bf16[512,512]{1,0:T(8,128)(2,1)}, u32[]{:S(2)}) copy-start(bf16[512,512]{1,0:T(8,128)(2,1)} %param.12) | copy-start | bytes 1572868
  6.5 28.8 %all-gather.2.cloned.1.call-start = ((), (), s32[]{:S(2)}) async-start(), calls=%async_computation.2 | async-start | bytes 1179648 | tf_op jit(solution)/shard_map/all_gather | solution.py:14
  7.3 660.4 %reduce-scatter.3.cloned.1.call-start = ((), (), s32[]{:S(2)}) async-start(), calls=%async_computation.3 | async-start | bytes 9437184 | tf_op jit(solution)/shard_map/reduce_scatter | solution.py:50
  35.3 4.3 copy-start.1
  275.5 421.8 %reduce-scatter.5.cloned.1.call-start = ((), (), s32[]{:S(2)}) async-start(), calls=%async_computation.4 | async-start | bytes 1310720 | tf_op jit(solution)/shard_map/reduce_scatter | solution.py:51
Sparse Core Ops, SparseCore 0:
  9.2 26.0 all-gather.1
  275.7 391.9 reduce-scatter.2
  670.0 27.2 reduce-scatter.4
where the time goes:
time: 715 us; the launch traced here: 706 us
  waiting for transfers between devices  448 us (63%)
  loops' own time  107 us (15%)
  local copies, waits for them, and re-layouts  89.4 us (13%)
  matrix products  46.8 us (7%)
  between operations  13.1 us (2%)
    reduce_scatter x1, waiting for transfers between devices, body(): lax.psum_scatter(partial_value, 'feat', scatter_dimension=1, tiled=True)  392 us
    another operation x1, loops' own time, body(): partial_value = lax.fori_loop(0, live_tiles, add_tile, partial_value)  107 us
    dot_general x27, matrix products, add_tile(): jnp.dot(tile_cells.astype(jnp.bfloat16), source_msg, preferred_element_ty...  44.8 us
    dynamic_slice x54, local copies, waits for them, and re-layouts, add_tile(): lax.dynamic_slice_in_dim(running, target * tile_size, tile_size, 0)  34.5 us
    dynamic_update_slice x54, local copies, waits for them, and re-layouts, add_tile(): lax.dynamic_update_slice_in_dim(running, current + contribution, target *...  29.2 us
    reduce_scatter x1, waiting for transfers between devices, body(): reduced = lax.psum_scatter(narrowed, 'dom', scatter_dimension=0, tiled=True)  28.8 us
    all_gather x1, waiting for transfers between devices, body(): features = lax.all_gather(node_feats, 'feat', axis=1, tiled=True)  26.6 us
    dynamic_slice x27, local copies, waits for them, and re-layouts, add_tile(): source = tile_list[slot_index, 2]  17.8 us
  transfers between devices with their start and end apart: 3, of which 3 were waited for; matrix products, arithmetic and copies ran while one was open for 0% of the time, Pallas kernels for 0%

commit v1 on v0

v1 whole, which is shorter than its diff:
```python
import functools

import jax
import jax.numpy as jnp
from jax import lax
from jax.experimental import pallas as pl
from jax.experimental.pallas import tpu as pltpu
from jax.sharding import PartitionSpec as P

MESH = pl.DeviceIdType.MESH
VMEM_LIMIT = 60 * 1024 * 1024


def bit_count(size):
    count = size.bit_length() - 1
    assert 1 << count == size
    return count


def flips(count):
    me = lax.axis_index("feat")
    bits = [(me // (1 << b)) % 2 for b in range(count)]
    return me, bits, [(1 - 2 * bits[b]) * (1 << b) for b in range(count)]


def orders(count, chunks):
    rest = list(range(1, count))
    return [[0] + (rest if c % 2 == 0 else rest[::-1]) for c in range(chunks)]


def greet(feat_partners, dom_partners):
    barrier = pltpu.get_barrier_semaphore()
    dom = lax.axis_index("dom")
    me = lax.axis_index("feat")
    for partner in feat_partners:
        pl.semaphore_signal(barrier, inc=1, device_id=(dom, partner), device_id_type=MESH)
    for partner in dom_partners:
        pl.semaphore_signal(barrier, inc=1, device_id=(partner, me), device_id_type=MESH)
    pl.semaphore_wait(barrier, len(feat_partners) + len(dom_partners))


def message_kernel(
    n, feats_ref, rel_ref, self_ref, bias_ref, degree_ref, msg_ref, own_ref,
    gathered, rel_t, self_t, bias_t, send_sem, recv_sem,
):
    count = bit_count(n)
    relations = rel_ref.shape[0]
    chunks, _, width, tile = gathered.shape
    hidden = n * width
    me, bits, step = flips(count)
    dom = lax.axis_index("dom")
    plan = [order[::-1] for order in orders(count, chunks)]

    for c in range(chunks):
        block = feats_ref[c * tile:(c + 1) * tile, :].astype(jnp.float32)
        gathered[c, me] = block.T.astype(jnp.bfloat16)
    greet([me + step[b] for b in range(count)], [])

    def held(order, stage):
        owners = [me]
        for b in order[:stage]:
            owners = owners + [owner + step[b] for owner in owners]
        return owners

    started = []

    def send(c, stage):
        order = plan[c]
        partner = me + step[order[stage]]
        for i, owner in enumerate(held(order, stage)):
            copy = pltpu.make_async_remote_copy(
                src_ref=gathered.at[c, owner],
                dst_ref=gathered.at[c, owner],
                send_sem=send_sem.at[c, (1 << stage) - 1 + i],
                recv_sem=recv_sem.at[c, (1 << stage) - 1 + i],
                device_id=(dom, partner),
                device_id_type=MESH,
            )
            copy.start()
            started.append(copy)

    def receive(c, stage):
        order = plan[c]
        for i, owner in enumerate(held(order, stage)):
            arrived = owner + step[order[stage]]
            pltpu.make_async_remote_copy(
                src_ref=gathered.at[c, arrived],
                dst_ref=gathered.at[c, arrived],
                send_sem=send_sem.at[c, (1 << stage) - 1 + i],
                recv_sem=recv_sem.at[c, (1 << stage) - 1 + i],
                device_id=(dom, me + step[order[stage]]),
                device_id_type=MESH,
            ).wait_recv()

    for c in range(chunks):
        send(c, 0)
    for r in range(relations):
        rel_t[r] = rel_ref[r].T
    self_t[...] = self_ref[...].T
    bias_t[...] = jnp.broadcast_to(bias_ref[...], (128, hidden)).T
    for stage in range(count):
        for c in range(chunks):
            receive(c, stage)
            if stage + 1 < count:
                send(c, stage + 1)
    self_rows = self_t[pl.ds(pl.multiple_of(me * width, width), width), :]
    bias_column = bias_t[pl.ds(pl.multiple_of(me * width, width), width), :][:, :1]
    for c in range(chunks):
        features = gathered[c].reshape(hidden, tile)
        own_ref[c] = (
            jnp.dot(self_rows, features, preferred_element_type=jnp.float32) + bias_column
        )
        for r in range(relations):
            degree = degree_ref[r:r + 1, c * tile:(c + 1) * tile]
            factor = 1.0 / jnp.maximum(degree, 1).astype(jnp.float32)
            product = jnp.dot(rel_t[r], features, preferred_element_type=jnp.float32)
            msg_ref[r * chunks + c] = (product * factor).astype(jnp.bfloat16)
    for copy in started:
        copy.wait_send()


def tile_kernel(n, chunks, index_ref, count_ref, tiles_ref, msg_ref, out_ref, acc):
    step = pl.program_id(0)
    per_step = tiles_ref.shape[0]
    bits = bit_count(n)
    blocks, hidden, tile = acc.shape
    width = hidden // n

    @pl.when(step == 0)
    def _():
        acc[...] = jnp.zeros_like(acc)

    for i in range(per_step):
        slot = step * per_step + i
        live = (slot < count_ref[0, 0]).astype(jnp.int32)
        message = msg_ref[index_ref[slot, 0] * chunks + index_ref[slot, 2]]
        cells = (tiles_ref[i] * live).astype(jnp.float32).astype(jnp.bfloat16)
        target = index_ref[slot, 1]
        acc[target] += lax.dot_general(
            message, cells, (((1,), (1,)), ((), ())), preferred_element_type=jnp.float32
        )

    @pl.when(step == pl.num_programs(0) - 1)
    def _():
        plan = orders(bits, chunks)

        def write(g, carry):
            for c in range(chunks):
                for f in range(n):
                    place = 0
                    for b in plan[c]:
                        place = place * 2 + (f >> b) % 2
                    part = acc[g * chunks + c, f * width:(f + 1) * width, :]
                    out_ref[c, place, g] = part.astype(jnp.bfloat16)
            return carry

        lax.fori_loop(0, blocks // chunks, write, 0)


def reduce_kernel(n, groups, part_ref, own_ref, out_ref, *scratch):
    count = bit_count(n)
    landed, crossed = scratch[:count], scratch[count]
    send_sem, recv_sem, cross_send, cross_recv = scratch[count + 1:]
    chunks, _, _, width, tile = part_ref.shape
    me, bits, step = flips(count)
    dom = lax.axis_index("dom")
    peers = [lax.rem(dom + k, groups) for k in range(1, groups)]
    plan = orders(count, chunks)
    greet([me + step[b] for b in range(count)], peers)
    started = []

    def source(c, stage):
        return part_ref.at[c] if stage == 0 else landed[stage - 1].at[c]

    def copy_of(c, stage):
        b = plan[c][stage]
        half = n >> (stage + 1)
        return pltpu.make_async_remote_copy(
            src_ref=source(c, stage).at[pl.ds((1 - bits[b]) * half, half)],
            dst_ref=landed[stage].at[c],
            send_sem=send_sem.at[c, stage],
            recv_sem=recv_sem.at[c, stage],
            device_id=(dom, me + step[b]),
            device_id_type=MESH,
        )

    def cross_of(c, k):
        return pltpu.make_async_remote_copy(
            src_ref=landed[count - 1].at[c, 0, peers[k]],
            dst_ref=crossed.at[c, k],
            send_sem=cross_send.at[c, k],
            recv_sem=cross_recv.at[c, k],
            device_id=(peers[k], me),
            device_id_type=MESH,
        )

    def begin(copy):
        copy.start()
        started.append(copy)

    for c in range(chunks):
        begin(copy_of(c, 0))
    for stage in range(count):
        half = n >> (stage + 1)
        for c in range(chunks):
            copy_of(c, stage).wait_recv()
            kept = bits[plan[c][stage]] * half
            for i in range(half):
                def add(g, carry, c=c, i=i, kept=kept, stage=stage):
                    mine = source(c, stage)[kept + i, g].astype(jnp.float32)
                    total = mine + landed[stage][c, i, g].astype(jnp.float32)
                    landed[stage][c, i, g] = total.astype(jnp.bfloat16)
                    return carry

                lax.fori_loop(0, groups, add, 0)
            if stage + 1 < count:
                begin(copy_of(c, stage + 1))
            else:
                for k in range(groups - 1):
                    begin(cross_of(c, k))
    for c in range(chunks):
        total = own_ref[c] + landed[count - 1][c, 0, dom].astype(jnp.float32)
        for k in range(groups - 1):
            cross_of(c, k).wait_recv()
            total = total + crossed[c, k].astype(jnp.float32)
        out_ref[c * tile:(c + 1) * tile, :] = total.T.astype(jnp.bfloat16)
    for copy in started:
        copy.wait_send()


def body(n, groups, node_feats, rel_weight, self_weight, bias, out_degree, adjacency, tile_index, tile_count):
    owned, width = node_feats.shape
    relations, hidden, _ = rel_weight.shape
    slots, tile = adjacency.shape[2], adjacency.shape[-1]
    chunks = owned // tile
    count = bit_count(n)
    whole = pl.BlockSpec(memory_space=pltpu.VMEM)
    messages, own = pl.pallas_call(
        functools.partial(message_kernel, n),
        out_shape=(
            jax.ShapeDtypeStruct((relations * chunks, hidden, tile), jnp.bfloat16),
            jax.ShapeDtypeStruct((chunks, width, tile), jnp.float32),
        ),
        in_specs=[whole] * 5,
        out_specs=(whole, whole),
        scratch_shapes=[
            pltpu.VMEM((chunks, n, width, tile), jnp.bfloat16),
            pltpu.VMEM((relations, hidden, hidden), jnp.bfloat16),
            pltpu.VMEM((hidden, hidden), jnp.bfloat16),
            pltpu.VMEM((hidden, 128), jnp.float32),
            pltpu.SemaphoreType.DMA((chunks, n)),
            pltpu.SemaphoreType.DMA((chunks, n)),
        ],
        compiler_params=pltpu.CompilerParams(
            collective_id=0, has_side_effects=True, vmem_limit_bytes=VMEM_LIMIT
        ),
        name="messages",
    )(node_feats, rel_weight, self_weight, bias[None, :], out_degree)

    per_step = 4 if slots % 4 == 0 else 1
    partial = pl.pallas_call(
        functools.partial(tile_kernel, n, chunks),
        grid=(slots // per_step,),
        out_shape=jax.ShapeDtypeStruct((chunks, n, groups, width, tile), jnp.bfloat16),
        in_specs=[
            pl.BlockSpec(memory_space=pltpu.SMEM),
            pl.BlockSpec(memory_space=pltpu.SMEM),
            pl.BlockSpec((per_step, tile, tile), lambda i: (i, 0, 0)),
            whole,
        ],
        out_specs=whole,
        scratch_shapes=[pltpu.VMEM((groups * chunks, hidden, tile), jnp.float32)],
        compiler_params=pltpu.CompilerParams(vmem_limit_bytes=VMEM_LIMIT),
        name="tiles",
    )(tile_index[0, 0], tile_count, adjacency[0, 0], messages)

    landed = [
        pltpu.VMEM((chunks, n >> (stage + 1), groups, width, tile), jnp.bfloat16)
        for stage in range(count)
    ]
    return pl.pallas_call(
        functools.partial(reduce_kernel, n, groups),
        out_shape=jax.ShapeDtypeStruct((owned, width), jnp.bfloat16),
        in_specs=[whole] * 2,
        out_specs=whole,
        scratch_shapes=landed + [
            pltpu.VMEM((chunks, groups - 1, width, tile), jnp.bfloat16),
            pltpu.SemaphoreType.DMA((chunks, count)),
            pltpu.SemaphoreType.DMA((chunks, count)),
            pltpu.SemaphoreType.DMA((chunks, groups - 1)),
            pltpu.SemaphoreType.DMA((chunks, groups - 1)),
        ],
        compiler_params=pltpu.CompilerParams(
            collective_id=1, has_side_effects=True, vmem_limit_bytes=VMEM_LIMIT
        ),
        name="reduce",
    )(partial, own)


def solution(mesh):
    placed = (
        P("dom", "feat"),
        P(),
        P(),
        P(),
        P(None, "dom"),
        P("dom", "feat", None, None, None),
        P("dom", "feat", None, None),
        P("dom", "feat"),
    )
    return jax.shard_map(
        functools.partial(body, mesh.shape["feat"], mesh.shape["dom"]),
        mesh=mesh, in_specs=placed, out_specs=P("dom", "feat"), check_vma=False,
    )
```

time: 715 us -> 80.8 us (0.11); the launches traced: 706 us -> 80.3 us
  waiting for transfers between devices: 448 us -> 0 us
  loops' own time: 107 us -> 0 us
  local copies, waits for them, and re-layouts: 89.4 us -> 4.84 us
  Pallas kernels: 0 us -> 74.8 us
  matrix products: 46.8 us -> 0 us
  between operations: 13.1 us -> 0.67 us
    reduce_scatter x2 -> x0, waiting for transfers between devices: 421 us -> none  [the longest x1 392 us: body(): lax.psum_scatter(partial_value, 'feat', scatter_dimension=1, tiled=True)]
    another operation x1 -> x0, loops' own time: 107 us -> none  [body(): partial_value = lax.fori_loop(0, live_tiles, add_tile, partial_value)]
    pallas_call x0 -> x3, Pallas kernels: none -> 74.8 us  [the longest x1 38.1 us: body(): pl.pallas_call(functools.partial(reduce_kernel, n, groups), out_shape=jax...]
    dynamic_slice x109 -> x0, local copies, waits for them, and re-layouts: 55.2 us -> none  [the longest x54 34.5 us: add_tile(): lax.dynamic_slice_in_dim(running, target * tile_size, tile_size, 0)]
    dot_general x28 -> x0, matrix products: 46.8 us -> none  [the longest x27 44.8 us: add_tile(): jnp.dot(tile_cells.astype(jnp.bfloat16), source_msg, preferred_element_ty...]
    dynamic_update_slice x54 -> x0, local copies, waits for them, and re-layouts: 29.2 us -> none  [add_tile(): lax.dynamic_update_slice_in_dim(running, current + contribution, target *...]
    all_gather x1 -> x0, waiting for transfers between devices: 26.6 us -> none  [body(): features = lax.all_gather(node_feats, 'feat', axis=1, tiled=True)]
  transfers between devices with their start and end apart: 3 -> 0, of which waited for: 3 -> 0; matrix products, arithmetic and copies ran while one was open for 0% -> 0% of each run, Pallas kernels for 0% -> 0%
where the time goes in v1:
time: 80.8 us; the launch traced here: 80.3 us
  Pallas kernels  74.8 us (93%)
  local copies, waits for them, and re-layouts  4.84 us (6%)
    pallas_call x1, Pallas kernels, body(): pl.pallas_call(functools.partial(reduce_kernel, n, groups), out_shape=jax...  38.1 us
    pallas_call x1, Pallas kernels, body(): pl.pallas_call(functools.partial(tile_kernel, n, chunks), grid=(slots //...  19.7 us
    pallas_call x1, Pallas kernels, body(): pl.pallas_call(functools.partial(message_kernel, n), out_shape=(jax.Shape...  17 us
    unnamed x2, local copies, waits for them, and re-layouts  3.12 us
    pallas_call x1, local copies, waits for them, and re-layouts, body(): pl.pallas_call(functools.partial(reduce_kernel, n, groups), out_shape=jax...  1.73 us

profile of v1, /device:TPU:0, one launch (start us, length us, event | category | flops | bytes accessed | tf_op | source)
XLA Modules:
  0.0 80.3 jit_solution(8733122380661221102)
XLA Ops:
  0.7 1.4 %copy.9 = s32[1,1,64,3]{3,2,1,0:T(8,128)} copy(s32[1,1,64,3]{2,1,3,0:T(1,128)} %param.14) | data formatting | bytes 1536 | tf_op args[6]
  2.0 1.7 %copy.10.feats_ref = bf16[1024,64]{1,0:T(8,128)(2,1)} copy(bf16[1024,64]{0,1:T(8,128)(2,1)} %param.8) | data formatting | bytes 262144 | tf_op args[0]
  3.8 17.0 %messages.1 = (bf16[16,512,256]{2,1,0:T(8,128)(2,1)}, f32[4,64,256]{2,1,0:T(8,128)}) custom-call(bf16[1024,64]{1,0:T(8,128)(2,1)} %copy.10.feats_ref, bf16[4,512,512]{2,1,0:T(8,128)(2,1)} %rel_ref.1, bf16[512,512]{1,0:T(8,128)(2,1)} %self_ref.1, f32[1,512]{1,0:T(1,128)} %bitcast.5, s32[4,1024]{1,0:T(4,128)} %degree_ref.1), custom_call_target="tpu_custom_call" | custom-call | tf_op jit(solution)/shard_map/messages/pallas_call | solution.py:238
  20.8 19.7 %tiles.1.part_ref = bf16[4,8,4,64,256]{4,3,2,1,0:T(8,128)(2,1)} custom-call(s32[64,3]{1,0:T(8,128)} %bitcast.4, s32[1,1]{1,0:T(1,128)S(6)} %copy.12.count_ref, s32[64,256,256]{2,1,0:T(8,128)} %bitcast.3, bf16[16,512,256]{2,1,0:T(8,128)(2,1)} %get-tuple-element.7.msg_ref), custom_call_target="tpu_custom_call" | custom-call | tf_op jit(solution)/shard_map/tiles/pallas_call | solution.py:261
  40.5 38.1 %reduce.1 = bf16[1024,64]{1,0:T(8,128)(2,1)} custom-call(bf16[4,8,4,64,256]{4,3,2,1,0:T(8,128)(2,1)} %tiles.1.part_ref, f32[4,64,256]{2,1,0:T(8,128)} %get-tuple-element.8.own_ref), custom_call_target="tpu_custom_call" | custom-call | tf_op jit(solution)/shard_map/reduce/pallas_call | solution.py:281
  78.6 1.7 %copy.11 = bf16[1024,64]{0,1:T(8,128)(2,1)} copy(bf16[1024,64]{1,0:T(8,128)(2,1)} %reduce.1) | data formatting | bytes 262144 | tf_op jit(solution)/shard_map/reduce/pallas_call | solution.py:281

commit v2 on v1

v2 whole, which is shorter than its diff:
```python
import functools

import jax
import jax.numpy as jnp
from jax import lax
from jax.experimental import pallas as pl
from jax.experimental.pallas import tpu as pltpu
from jax.sharding import PartitionSpec as P

MESH = pl.DeviceIdType.MESH
VMEM_LIMIT = 60 * 1024 * 1024


def bit_count(size):
    count = size.bit_length() - 1
    assert 1 << count == size
    return count


def flips(count):
    me = lax.axis_index("feat")
    bits = [(me // (1 << b)) % 2 for b in range(count)]
    return me, bits, [(1 - 2 * bits[b]) * (1 << b) for b in range(count)]


def orders(count, chunks):
    rest = list(range(1, count))
    return [[0] + (rest if c % 2 == 0 else rest[::-1]) for c in range(chunks)]


def greet(partners):
    barrier = pltpu.get_barrier_semaphore()
    dom = lax.axis_index("dom")
    for partner in partners:
        pl.semaphore_signal(barrier, inc=1, device_id=(dom, partner), device_id_type=MESH)
    pl.semaphore_wait(barrier, len(partners))


def message_kernel(
    n, feats_ref, rel_ref, self_ref, bias_ref, degree_ref, msg_ref, own_ref,
    gathered, rel_t, self_t, bias_t, send_sem, recv_sem,
):
    count = bit_count(n)
    relations = rel_ref.shape[0]
    chunks, _, width, tile = gathered.shape
    hidden = n * width
    me, bits, step = flips(count)
    dom = lax.axis_index("dom")
    plan = [order[::-1] for order in orders(count, chunks)]

    for c in range(chunks):
        gathered[c, me] = feats_ref[:, c * tile:(c + 1) * tile]
    greet([me + step[b] for b in range(count)])

    def held(order, stage):
        owners = [me]
        for b in order[:stage]:
            owners = owners + [owner + step[b] for owner in owners]
        return owners

    started = []

    def send(c, stage):
        order = plan[c]
        partner = me + step[order[stage]]
        for i, owner in enumerate(held(order, stage)):
            copy = pltpu.make_async_remote_copy(
                src_ref=gathered.at[c, owner],
                dst_ref=gathered.at[c, owner],
                send_sem=send_sem.at[c, (1 << stage) - 1 + i],
                recv_sem=recv_sem.at[c, (1 << stage) - 1 + i],
                device_id=(dom, partner),
                device_id_type=MESH,
            )
            copy.start()
            started.append(copy)

    def receive(c, stage):
        order = plan[c]
        for i, owner in enumerate(held(order, stage)):
            arrived = owner + step[order[stage]]
            pltpu.make_async_remote_copy(
                src_ref=gathered.at[c, arrived],
                dst_ref=gathered.at[c, arrived],
                send_sem=send_sem.at[c, (1 << stage) - 1 + i],
                recv_sem=recv_sem.at[c, (1 << stage) - 1 + i],
                device_id=(dom, me + step[order[stage]]),
                device_id_type=MESH,
            ).wait_recv()

    for c in range(chunks):
        send(c, 0)
    for r in range(relations):
        rel_t[r] = rel_ref[r].T
    self_t[...] = self_ref[...].T
    bias_t[...] = jnp.broadcast_to(bias_ref[...], (128, hidden)).T
    self_rows = self_t[pl.ds(pl.multiple_of(me * width, width), width), :]
    bias_column = bias_t[pl.ds(pl.multiple_of(me * width, width), width), :][:, :1]
    for stage in range(count):
        for c in range(chunks):
            receive(c, stage)
            if stage + 1 < count:
                send(c, stage + 1)
                continue
            features = gathered[c].reshape(hidden, tile)
            own_ref[c] = (
                jnp.dot(self_rows, features, preferred_element_type=jnp.float32) + bias_column
            )
            for r in range(relations):
                degree = degree_ref[r:r + 1, c * tile:(c + 1) * tile]
                factor = 1.0 / jnp.maximum(degree, 1).astype(jnp.float32)
                product = jnp.dot(rel_t[r], features, preferred_element_type=jnp.float32)
                msg_ref[r * chunks + c] = (product * factor).astype(jnp.bfloat16)
    for copy in started:
        copy.wait_send()


def reduce_orders(n, groups, chunks):
    rest = [("feat", b) for b in range(1, bit_count(n))]
    last = [("dom", b) for b in range(bit_count(groups))]
    rest, last = rest + last[:1], last[1:]
    plans = []
    for c in range(chunks):
        k = c % max(len(rest), 1)
        plans.append([("feat", 0)] + rest[k:] + rest[:k] + last)
    return plans


def tile_kernel(n, groups, chunks, index_ref, count_ref, tiles_ref, msg_ref, sent_ref, kept_ref, acc):
    step = pl.program_id(0)
    per_step = tiles_ref.shape[0]
    blocks, hidden, tile = acc.shape
    sources = blocks // groups
    width = hidden // n
    lanes = sent_ref.shape[-1]
    pieces = tile // lanes
    parity = lax.rem(lax.axis_index("feat"), 2)

    @pl.when(step == 0)
    def _():
        acc[...] = jnp.zeros_like(acc)

    for i in range(per_step):
        slot = step * per_step + i
        live = (slot < count_ref[0, 0]).astype(jnp.int32)
        message = msg_ref[index_ref[0, 0, slot] * sources + index_ref[2, 0, slot]]
        cells = (tiles_ref[i] * live).astype(jnp.float32).astype(jnp.bfloat16)
        target = index_ref[1, 0, slot]
        acc[target] += lax.dot_general(
            message, cells, (((1,), (1,)), ((), ())), preferred_element_type=jnp.float32
        )

    @pl.when(step == pl.num_programs(0) - 1)
    def _():
        plans = reduce_orders(n, groups, chunks)
        for c in range(chunks):
            s, piece = c // pieces, c % pieces
            for g in range(groups):
                for f in range(0, n, 2):
                    place = 0
                    for axis, b in plans[c][1:]:
                        place = place * 2 + ((f if axis == "feat" else g) >> b) % 2
                    for ref, core in ((sent_ref, 1 - parity), (kept_ref, parity)):
                        start = pl.multiple_of((f + core) * width, width)
                        part = acc[
                            g * sources + s, pl.ds(start, width),
                            piece * lanes:(piece + 1) * lanes,
                        ]
                        ref[c, place] = part.astype(ref.dtype)


def reduce_kernel(n, groups, first_ref, kept_ref, own_ref, out_ref, total, *scratch):
    plans = reduce_orders(n, groups, first_ref.shape[0])
    stages = len(plans[0])
    landed, sent = scratch[:stages], (first_ref,) + scratch[stages:2 * stages - 1]
    send_sem, recv_sem = scratch[2 * stages - 1:]
    chunks, half_all, width, lanes = first_ref.shape
    tile = own_ref.shape[-1]
    pieces = tile // lanes
    me, dom = lax.axis_index("feat"), lax.axis_index("dom")

    def bit(axis, b):
        return ((me if axis == "feat" else dom) // (1 << b)) % 2

    def partner(axis, b):
        move = (1 - 2 * bit(axis, b)) * (1 << b)
        return (dom, me + move) if axis == "feat" else (dom + move, me)

    barrier = pltpu.get_barrier_semaphore()
    for axis, b in plans[0]:
        pl.semaphore_signal(barrier, inc=1, device_id=partner(axis, b), device_id_type=MESH)
    pl.semaphore_wait(barrier, stages)

    def copy_of(c, stage):
        return pltpu.make_async_remote_copy(
            src_ref=sent[stage].at[c],
            dst_ref=landed[stage].at[c],
            send_sem=send_sem.at[c, stage],
            recv_sem=recv_sem.at[c, stage],
            device_id=partner(*plans[c][stage]),
            device_id_type=MESH,
        )

    def arrived(stage, c, i):
        return landed[stage][c, i].astype(jnp.float32)

    for c in range(chunks):
        copy_of(c, 0).start()
    base = [0] * chunks
    for stage in range(stages):
        source = kept_ref if stage == 0 else total
        half = half_all >> (stage + 1)
        for c in range(chunks):
            copy_of(c, stage).wait_recv()
            if stage + 1 < stages:
                mine = bit(*plans[c][stage + 1])
                away = (1 - mine) * half
                stay = mine * half

                def give(i, carry, c=c, stage=stage, away=away, source=source):
                    value = source[c, base[c] + away + i] + arrived(stage, c, away + i)
                    sent[stage + 1][c, i] = value.astype(jnp.bfloat16)
                    return carry

                def keep(i, carry, c=c, stage=stage, stay=stay, source=source):
                    place = base[c] + stay + i
                    total[c, place] = source[c, place] + arrived(stage, c, stay + i)
                    return carry

                lax.fori_loop(0, half, give, 0, unroll=min(half, 4))
                copy_of(c, stage + 1).start()
                lax.fori_loop(0, half, keep, 0, unroll=min(half, 4))
                base[c] = base[c] + stay
            else:
                s, piece = c // pieces, c % pieces
                value = source[c, base[c]] + arrived(stage, c, 0)
                value = value + own_ref[s, :, piece * lanes:(piece + 1) * lanes]
                out_ref[:, c * lanes:(c + 1) * lanes] = value.astype(jnp.bfloat16)
    for stage in range(stages):
        for c in range(chunks):
            copy_of(c, stage).wait_send()


def body(n, groups, node_feats, rel_weight, self_weight, bias, out_degree, adjacency, tile_index, tile_count):
    owned, width = node_feats.shape
    relations, hidden, _ = rel_weight.shape
    slots, tile = adjacency.shape[2], adjacency.shape[-1]
    chunks = owned // tile
    count = bit_count(n)
    whole = pl.BlockSpec(memory_space=pltpu.VMEM)
    messages, own = pl.pallas_call(
        functools.partial(message_kernel, n),
        out_shape=(
            jax.ShapeDtypeStruct((relations * chunks, hidden, tile), jnp.bfloat16),
            jax.ShapeDtypeStruct((chunks, width, tile), jnp.float32),
        ),
        in_specs=[whole] * 5,
        out_specs=(whole, whole),
        scratch_shapes=[
            pltpu.VMEM((chunks, n, width, tile), jnp.bfloat16),
            pltpu.VMEM((relations, hidden, hidden), jnp.bfloat16),
            pltpu.VMEM((hidden, hidden), jnp.bfloat16),
            pltpu.VMEM((hidden, 128), jnp.float32),
            pltpu.SemaphoreType.DMA((chunks, n)),
            pltpu.SemaphoreType.DMA((chunks, n)),
        ],
        compiler_params=pltpu.CompilerParams(
            collective_id=0, has_side_effects=True, vmem_limit_bytes=VMEM_LIMIT
        ),
        name="messages",
    )(node_feats.T, rel_weight, self_weight, bias[None, :], out_degree)

    per_step = 4 if slots % 4 == 0 else 1
    lanes = tile // 2
    pieces = chunks * (tile // lanes)
    half = n * groups // 2
    sent, kept = pl.pallas_call(
        functools.partial(tile_kernel, n, groups, pieces),
        grid=(slots // per_step,),
        out_shape=(
            jax.ShapeDtypeStruct((pieces, half, width, lanes), jnp.bfloat16),
            jax.ShapeDtypeStruct((pieces, half, width, lanes), jnp.float32),
        ),
        in_specs=[
            pl.BlockSpec(memory_space=pltpu.SMEM),
            pl.BlockSpec(memory_space=pltpu.SMEM),
            pl.BlockSpec((per_step, tile, tile), lambda i: (i, 0, 0)),
            whole,
        ],
        out_specs=(whole, whole),
        scratch_shapes=[pltpu.VMEM((groups * chunks, hidden, tile), jnp.float32)],
        compiler_params=pltpu.CompilerParams(vmem_limit_bytes=VMEM_LIMIT),
        name="tiles",
    )(jnp.transpose(tile_index[0], (2, 0, 1)), tile_count, adjacency[0, 0], messages)

    stages = bit_count(n * groups)
    halves = [
        pltpu.VMEM((pieces, half >> stage, width, lanes), jnp.bfloat16)
        for stage in range(stages)
    ]
    result = pl.pallas_call(
        functools.partial(reduce_kernel, n, groups),
        out_shape=jax.ShapeDtypeStruct((width, owned), jnp.bfloat16),
        in_specs=[whole] * 3,
        out_specs=whole,
        scratch_shapes=[pltpu.VMEM((pieces, half, width, lanes), jnp.float32)]
        + halves + halves[1:] + [
            pltpu.SemaphoreType.DMA((pieces, stages)),
            pltpu.SemaphoreType.DMA((pieces, stages)),
        ],
        compiler_params=pltpu.CompilerParams(
            collective_id=1, has_side_effects=True, vmem_limit_bytes=VMEM_LIMIT
        ),
        name="reduce",
    )(sent, kept, own)
    return result.T


def solution(mesh):
    placed = (
        P("dom", "feat"),
        P(),
        P(),
        P(),
        P(None, "dom"),
        P("dom", "feat", None, None, None),
        P("dom", "feat", None, None),
        P("dom", "feat"),
    )
    return jax.shard_map(
        functools.partial(body, mesh.shape["feat"], mesh.shape["dom"]),
        mesh=mesh, in_specs=placed, out_specs=P("dom", "feat"), check_vma=False,
    )
```

time: 80.8 us -> 72.3 us (0.89)
  Pallas kernels: 74.8 us -> 69.7 us
  local copies, waits for them, and re-layouts: 4.84 us -> 1.57 us
    pallas_call x1, Pallas kernels: 38.1 us -> 31.8 us  [body(): pl.pallas_call(functools.partial(reduce_kernel, n, groups), out_shape=jax...]
    pallas_call x1 -> x0, local copies, waits for them, and re-layouts: 1.73 us -> none  [body(): pl.pallas_call(functools.partial(reduce_kernel, n, groups), out_shape=jax...]
    unnamed x2 -> x1, local copies, waits for them, and re-layouts: 3.12 us -> 1.57 us
where the time goes in v2:
time: 72.3 us; the launch traced here: 71.9 us
  Pallas kernels  69.7 us (96%)
  local copies, waits for them, and re-layouts  1.57 us (2%)
    pallas_call x1, Pallas kernels, body(): pl.pallas_call(functools.partial(reduce_kernel, n, groups), out_shape=jax...  31.8 us
    pallas_call x1, Pallas kernels, body(): pl.pallas_call(functools.partial(tile_kernel, n, groups, pieces), grid=(s...  20.5 us
    pallas_call x1, Pallas kernels, body(): pl.pallas_call(functools.partial(message_kernel, n), out_shape=(jax.Shape...  17.4 us
    unnamed x1, local copies, waits for them, and re-layouts  1.57 us

profile of v2, /device:TPU:0, one launch (start us, length us, event | category | flops | bytes accessed | tf_op | source)
XLA Modules:
  0.0 71.9 jit_solution(13554448264026149557)
XLA Ops:
  0.7 17.4 %messages.1 = (bf16[16,512,256]{2,1,0:T(8,128)(2,1)}, f32[4,64,256]{2,1,0:T(8,128)}) custom-call(bf16[64,1024]{1,0:T(8,128)(2,1)} %bitcast.9, bf16[4,512,512]{2,1,0:T(8,128)(2,1)} %rel_ref.1, bf16[512,512]{1,0:T(8,128)(2,1)} %self_ref.1, f32[1,512]{1,0:T(1,128)} %bitcast.10, s32[4,1024]{1,0:T(4,128)} %degree_ref.1), custom_call_target="tpu_custom_call" | custom-call | tf_op jit(solution)/shard_map/messages/pallas_call | solution.py:251
  18.1 20.5 %tiles.1 = (bf16[8,16,64,128]{3,2,1,0:T(8,128)(2,1)}, f32[8,16,64,128]{3,2,1,0:T(8,128)}) custom-call(s32[3,1,64]{2,1,0:T(1,128)} %bitcast.11, s32[1,1]{1,0:T(1,128)S(6)} %copy.10.count_ref, s32[64,256,256]{2,1,0:T(8,128)} %bitcast.7, bf16[16,512,256]{2,1,0:T(8,128)(2,1)} %get-tuple-element.9.msg_ref), custom_call_target="tpu_custom_call" | custom-call | tf_op jit(solution)/shard_map/tiles/pallas_call | solution.py:277
  38.6 31.8 %reduce.1 = bf16[64,1024]{1,0:T(8,128)(2,1)} custom-call(bf16[8,16,64,128]{3,2,1,0:T(8,128)(2,1)} %get-tuple-element.10.first_ref, f32[8,16,64,128]{3,2,1,0:T(8,128)} %get-tuple-element.11.kept_ref, f32[4,64,256]{2,1,0:T(8,128)} %get-tuple-element.12.own_ref), custom_call_target="tpu_custom_call" | custom-call | tf_op jit(solution)/shard_map/reduce/pallas_call | solution.py:301
  70.3 1.6 %copy.11 = bf16[1024,64]{0,1:T(8,128)(2,1)} copy(bf16[1024,64]{0,1:T(8,128)(2,1)} %bitcast.8) | data formatting | bytes 262144

commit v3 on v2

--- a/solution.py
+++ b/solution.py
@@ -8,7 +8,7 @@
 from jax.sharding import PartitionSpec as P
 
 MESH = pl.DeviceIdType.MESH
-VMEM_LIMIT = 60 * 1024 * 1024
+VMEM_LIMIT = 28 * 1024 * 1024
 
 
 def bit_count(size):
@@ -251,8 +251,8 @@
     messages, own = pl.pallas_call(
         functools.partial(message_kernel, n),
         out_shape=(
-            jax.ShapeDtypeStruct((relations * chunks, hidden, tile), jnp.bfloat16),
-            jax.ShapeDtypeStruct((chunks, width, tile), jnp.float32),
+            pltpu.VMEM((relations * chunks, hidden, tile), jnp.bfloat16),
+            pltpu.VMEM((chunks, width, tile), jnp.float32),
         ),
         in_specs=[whole] * 5,
         out_specs=(whole, whole),
@@ -270,7 +270,7 @@
         name="messages",
     )(node_feats.T, rel_weight, self_weight, bias[None, :], out_degree)
 
-    per_step = 4 if slots % 4 == 0 else 1
+    per_step = next(p for p in (8, 4, 2, 1) if slots % p == 0)
     lanes = tile // 2
     pieces = chunks * (tile // lanes)
     half = n * groups // 2
@@ -278,8 +278,8 @@
         functools.partial(tile_kernel, n, groups, pieces),
         grid=(slots // per_step,),
         out_shape=(
-            jax.ShapeDtypeStruct((pieces, half, width, lanes), jnp.bfloat16),
-            jax.ShapeDtypeStruct((pieces, half, width, lanes), jnp.float32),
+            pltpu.VMEM((pieces, half, width, lanes), jnp.bfloat16),
+            pltpu.VMEM((pieces, half, width, lanes), jnp.float32),
         ),
         in_specs=[
             pl.BlockSpec(memory_space=pltpu.SMEM),

time: 72.3 us -> 61.7 us (0.85)
  Pallas kernels: 69.7 us -> 54.4 us
  local copies, waits for them, and re-layouts: 1.57 us -> 6.26 us
    pallas_call x1, Pallas kernels: 20.5 us -> 12.4 us  [body(): pl.pallas_call(functools.partial(tile_kernel, n, groups, pieces), grid=(s...]
    unnamed x1 -> x13, local copies, waits for them, and re-layouts: 1.57 us -> 6.26 us
    pallas_call x1, Pallas kernels: 17.4 us -> 13.7 us  [body(): pl.pallas_call(functools.partial(message_kernel, n), out_shape=(pltpu.VME...]
    pallas_call x1, Pallas kernels: 31.8 us -> 28.3 us  [body(): pl.pallas_call(functools.partial(reduce_kernel, n, groups), out_shape=jax...]
where the time goes in v3:
time: 61.7 us; the launch traced here: 61.3 us
  Pallas kernels  54.4 us (88%)
  local copies, waits for them, and re-layouts  6.26 us (10%)
  between operations  0.7 us (1%)
    pallas_call x1, Pallas kernels, body(): pl.pallas_call(functools.partial(reduce_kernel, n, groups), out_shape=jax...  28.3 us
    pallas_call x1, Pallas kernels, body(): pl.pallas_call(functools.partial(message_kernel, n), out_shape=(pltpu.VME...  13.7 us
    pallas_call x1, Pallas kernels, body(): pl.pallas_call(functools.partial(tile_kernel, n, groups, pieces), grid=(s...  12.4 us
    unnamed x13, local copies, waits for them, and re-layouts  6.26 us

profile of v3, /device:TPU:0, one launch (start us, length us, event | category | flops | bytes accessed | tf_op | source)
XLA Modules:
  0.0 61.3 jit_solution(17074544386449128200)
XLA Ops:
  0.7 0.0 copy-start
  0.7 1.6 %copy-done = bf16[4,512,512]{2,1,0:T(8,128)(2,1)S(1)} copy-done((bf16[4,512,512]{2,1,0:T(8,128)(2,1)S(1)}, bf16[4,512,512]{2,1,0:T(8,128)(2,1)}, u32[]{:S(2)}) %copy-start) | copy-done | bytes 2097176
  2.2 0.0 copy-start.1
  2.2 1.0 %copy-done.1 = bf16[512,512]{1,0:T(8,128)(2,1)S(1)} copy-done((bf16[512,512]{1,0:T(8,128)(2,1)S(1)}, bf16[512,512]{1,0:T(8,128)(2,1)}, u32[]{:S(2)}) %copy-start.1) | copy-done | bytes 524312
  3.3 0.0 copy-start.2
  3.3 0.9 %copy-done.2 = bf16[1024,64]{0,1:T(8,128)(2,1)S(1)} copy-done((bf16[1024,64]{0,1:T(8,128)(2,1)S(1)}, bf16[1024,64]{0,1:T(8,128)(2,1)}, u32[]{:S(2)}) %copy-start.2) | copy-done | bytes 131096
  4.2 0.0 copy-start.3
  4.2 0.7 %copy-done.3 = s32[4,1024]{1,0:T(4,128)S(1)} copy-done((s32[4,1024]{1,0:T(4,128)S(1)}, s32[4,1024]{1,0:T(4,128)}, u32[]{:S(2)}) %copy-start.3) | copy-done | bytes 16408
  4.9 0.0 copy-start.4
  4.9 0.7 %copy-done.4 = f32[512]{0:T(512)S(1)} copy-done((f32[512]{0:T(512)S(1)}, f32[512]{0:T(512)}, u32[]{:S(2)}) %copy-start.4) | copy-done | bytes 2072
  5.6 13.7 %messages.1 = (bf16[16,512,256]{2,1,0:T(8,128)(2,1)S(1)}, f32[4,64,256]{2,1,0:T(8,128)S(1)}) custom-call(bf16[64,1024]{1,0:T(8,128)(2,1)S(1)} %bitcast.8, bf16[4,512,512]{2,1,0:T(8,128)(2,1)S(1)} %copy-done, bf16[512,512]{1,0:T(8,128)(2,1)S(1)} %copy-done.1, f32[1,512]{1,0:T(1,128)S(1)} %bitcast.9, s32[4,1024]{1,0:T(4,128)S(1)} %copy-done.3), custom_call_target="tpu_custom_call" | custom-call | tf_op jit(solution)/shard_map/messages/pallas_call | solution.py:251
  19.3 0.0 copy-start.5
  19.3 0.7 %copy-done.5 = s32[1,1,64,3]{2,1,3,0:T(1,128)S(1)} copy-done((s32[1,1,64,3]{2,1,3,0:T(1,128)S(1)}, s32[1,1,64,3]{2,1,3,0:T(1,128)}, u32[]{:S(2)}) %copy-start.5) | copy-done | bytes 792
  19.9 12.4 %tiles.1 = (bf16[8,16,64,128]{3,2,1,0:T(8,128)(2,1)S(1)}, f32[8,16,64,128]{3,2,1,0:T(8,128)S(1)}) custom-call(s32[3,1,64]{2,1,0:T(1,128)S(1)} %bitcast.10, s32[1,1]{1,0:T(1,128)S(6)} %copy.10.count_ref, s32[64,256,256]{2,1,0:T(8,128)} %bitcast.11, bf16[16,512,256]{2,1,0:T(8,128)(2,1)S(1)} %get-tuple-element.9.msg_ref), custom_call_target="tpu_custom_call" | custom-call | tf_op jit(solution)/shard_map/tiles/pallas_call | solution.py:277
  32.3 28.3 %reduce.1 = bf16[64,1024]{1,0:T(8,128)(2,1)S(1)} custom-call(bf16[8,16,64,128]{3,2,1,0:T(8,128)(2,1)S(1)} %get-tuple-element.10.first_ref, f32[8,16,64,128]{3,2,1,0:T(8,128)S(1)} %get-tuple-element.11.kept_ref, f32[4,64,256]{2,1,0:T(8,128)S(1)} %get-tuple-element.12.own_ref), custom_call_target="tpu_custom_call" | custom-call | tf_op jit(solution)/shard_map/reduce/pallas_call | solution.py:301
  60.7 0.7 %copy.11 = bf16[1024,64]{0,1:T(8,128)(2,1)} copy(bf16[1024,64]{0,1:T(8,128)(2,1)S(1)} %bitcast.7) | data formatting | bytes 262144
Async XLA Ops:
  0.7 1.6 %copy-start = (bf16[4,512,512]{2,1,0:T(8,128)(2,1)S(1)}, bf16[4,512,512]{2,1,0:T(8,128)(2,1)}, u32[]{:S(2)}) copy-start(bf16[4,512,512]{2,1,0:T(8,128)(2,1)} %rel_ref.1) | copy-start | bytes 6291460
  2.2 1.0 %copy-start.1 = (bf16[512,512]{1,0:T(8,128)(2,1)S(1)}, bf16[512,512]{1,0:T(8,128)(2,1)}, u32[]{:S(2)}) copy-start(bf16[512,512]{1,0:T(8,128)(2,1)} %self_ref.1) | copy-start | bytes 1572868
  3.3 0.9 %copy-start.2 = (bf16[1024,64]{0,1:T(8,128)(2,1)S(1)}, bf16[1024,64]{0,1:T(8,128)(2,1)}, u32[]{:S(2)}) copy-start(bf16[1024,64]{0,1:T(8,128)(2,1)} %param.8) | copy-start | bytes 393220
  4.2 0.7 %copy-start.3 = (s32[4,1024]{1,0:T(4,128)S(1)}, s32[4,1024]{1,0:T(4,128)}, u32[]{:S(2)}) copy-start(s32[4,1024]{1,0:T(4,128)} %degree_ref.1) | copy-start | bytes 49156
  4.9 0.7 %copy-start.4 = (f32[512]{0:T(512)S(1)}, f32[512]{0:T(512)}, u32[]{:S(2)}) copy-start(f32[512]{0:T(512)} %param.11) | copy-start | bytes 6148
  19.3 0.7 %copy-start.5 = (s32[1,1,64,3]{2,1,3,0:T(1,128)S(1)}, s32[1,1,64,3]{2,1,3,0:T(1,128)}, u32[]{:S(2)}) copy-start(s32[1,1,64,3]{2,1,3,0:T(1,128)} %param.14) | copy-start | bytes 2308

commit v4 on v3

--- a/solution.py
+++ b/solution.py
@@ -268,7 +268,10 @@
             collective_id=0, has_side_effects=True, vmem_limit_bytes=VMEM_LIMIT
         ),
         name="messages",
-    )(node_feats.T, rel_weight, self_weight, bias[None, :], out_degree)
+    )(*[
+        pltpu.with_memory_space_constraint(x, pltpu.HBM)
+        for x in (node_feats.T, rel_weight, self_weight, bias[None, :], out_degree)
+    ])
 
     per_step = next(p for p in (8, 4, 2, 1) if slots % p == 0)
     lanes = tile // 2

time: 61.7 us -> 58.4 us (0.947)
  local copies, waits for them, and re-layouts: 6.26 us -> 1.33 us
  Pallas kernels: 54.4 us -> 56.1 us
    unnamed x13 -> x3, local copies, waits for them, and re-layouts: 6.26 us -> 1.33 us
    pallas_call x1, Pallas kernels: 13.7 us -> 15.4 us  [body(): pl.pallas_call(functools.partial(message_kernel, n), out_shape=(pltpu.VME...]
where the time goes in v4:
time: 58.4 us; the launch traced here: 58.1 us
  Pallas kernels  56.1 us (96%)
  local copies, waits for them, and re-layouts  1.33 us (2%)
  between operations  0.68 us (1%)
    pallas_call x1, Pallas kernels, body(): pl.pallas_call(functools.partial(reduce_kernel, n, groups), out_shape=jax...  28.3 us
    pallas_call x1, Pallas kernels, body(): pl.pallas_call(functools.partial(message_kernel, n), out_shape=(pltpu.VME...  15.4 us
    pallas_call x1, Pallas kernels, body(): pl.pallas_call(functools.partial(tile_kernel, n, groups, pieces), grid=(s...  12.4 us
    unnamed x3, local copies, waits for them, and re-layouts  1.33 us

profile of v4, /device:TPU:0, one launch (start us, length us, event | category | flops | bytes accessed | tf_op | source)
XLA Modules:
  0.0 58.1 jit_solution(14418904814682063626)
XLA Ops:
  0.7 15.4 %messages.1 = (bf16[16,512,256]{2,1,0:T(8,128)(2,1)S(1)}, f32[4,64,256]{2,1,0:T(8,128)S(1)}) custom-call(bf16[64,1024]{1,0:T(8,128)(2,1)} %bitcast.10, bf16[4,512,512]{2,1,0:T(8,128)(2,1)} %rel_ref.1, bf16[512,512]{1,0:T(8,128)(2,1)} %self_ref.1, f32[1,512]{1,0:T(1,128)} %bitcast.11, s32[4,1024]{1,0:T(4,128)} %degree_ref.1), custom_call_target="tpu_custom_call" | custom-call | tf_op jit(solution)/shard_map/messages/pallas_call | solution.py:251
  16.0 0.0 copy-start
  16.0 0.7 %copy-done = s32[1,1,64,3]{2,1,3,0:T(1,128)S(1)} copy-done((s32[1,1,64,3]{2,1,3,0:T(1,128)S(1)}, s32[1,1,64,3]{2,1,3,0:T(1,128)}, u32[]{:S(2)}) %copy-start) | copy-done | bytes 792
  16.7 12.4 %tiles.1 = (bf16[8,16,64,128]{3,2,1,0:T(8,128)(2,1)S(1)}, f32[8,16,64,128]{3,2,1,0:T(8,128)S(1)}) custom-call(s32[3,1,64]{2,1,0:T(1,128)S(1)} %bitcast.8, s32[1,1]{1,0:T(1,128)S(6)} %copy.10.count_ref, s32[64,256,256]{2,1,0:T(8,128)} %bitcast.9, bf16[16,512,256]{2,1,0:T(8,128)(2,1)S(1)} %get-tuple-element.9.msg_ref), custom_call_target="tpu_custom_call" | custom-call | tf_op jit(solution)/shard_map/tiles/pallas_call | solution.py:280
  29.1 28.3 %reduce.1 = bf16[64,1024]{1,0:T(8,128)(2,1)S(1)} custom-call(bf16[8,16,64,128]{3,2,1,0:T(8,128)(2,1)S(1)} %get-tuple-element.10.first_ref, f32[8,16,64,128]{3,2,1,0:T(8,128)S(1)} %get-tuple-element.11.kept_ref, f32[4,64,256]{2,1,0:T(8,128)S(1)} %get-tuple-element.12.own_ref), custom_call_target="tpu_custom_call" | custom-call | tf_op jit(solution)/shard_map/reduce/pallas_call | solution.py:304
  57.4 0.7 %copy.11 = bf16[1024,64]{0,1:T(8,128)(2,1)} copy(bf16[1024,64]{0,1:T(8,128)(2,1)S(1)} %bitcast.7) | data formatting | bytes 262144
Async XLA Ops:
  16.0 0.7 %copy-start = (s32[1,1,64,3]{2,1,3,0:T(1,128)S(1)}, s32[1,1,64,3]{2,1,3,0:T(1,128)}, u32[]{:S(2)}) copy-start(s32[1,1,64,3]{2,1,3,0:T(1,128)} %param.14) | copy-start | bytes 2308
